TPU v7x, 128 devices: a whole 4x4x4 slice. The times are simulated.
128 devices in a mesh: lat: 4 (over x_hi, core), lon: 4 (over z), lev: 8 (over y, x_lo).
Axes of the slice: x: 4 (x_hi: 2, x_lo: 2; x = x_hi * 2 + x_lo), y: 4, z: 4, core: 2. Of those that a mesh axis runs over, the one named last changes fastest.
Arguments:
- initial_heat: float32 [128, 512, 32, 128], P('lat', 'lon', 'lev'), may hold values from 0.5 to 2
- diffusivity_ratio: float32 [128, 512, 32, 128], P('lat', 'lon', 'lev'), may hold values from 0.03 to 0.15
- forcing_term: float32 [128, 512, 32, 128], P('lat', 'lon', 'lev'), may hold values from -0.2 to 0.2
Outputs:
- standard_deviation_score: float32 [128, 512, 32, 128], P('lat', 'lon', 'lev')
- temperature_end: float32 [128, 512, 32, 128], P('lat', 'lon', 'lev')
All inputs are finite; a program needn't handle non-finite values.
Results may differ from a plain program's by a relative error of at most 0.00002.
Values sent between devices are 32-bit elements; how exact they have to be, the bound alone decides.
No kernel may reach another device: no remote copies, remote signals or barrier semaphores. Data moves between devices by JAX's collectives and lax.ppermute only.
A program may use at most 128 MiB of HBM per device.

v0:
```python
import jax
import jax.numpy as jnp
from jax import lax
from jax.experimental import pallas as pl
from jax.experimental.pallas import tpu as pltpu
from jax.sharding import PartitionSpec as P


STEPS = 4
ROWS = 8
BAND = 4
CUT = 16


def shift(x, axis, by):
    size = lax.axis_size(axis)
    return lax.ppermute(x, axis, [(i, (i + by) % size) for i in range(size)])


def take_body(parts, whole, low_row, *refs):
    outs, sems = refs[:-1], refs[-1]
    copies = []
    for n, (out, part) in enumerate(zip(outs, parts)):
        copies += [
            pltpu.make_async_copy(source(whole, low_row[0]), target(out), sems.at[n, k])
            for k, (source, target) in enumerate(part)
        ]
    for copy in copies:
        copy.start()
    for copy in copies:
        copy.wait()


def take(whole, low_row, shapes, parts, limit=10):
    lanes = whole.shape[-1]
    got = pl.pallas_call(
        lambda *refs: take_body(parts, *refs),
        in_specs=[pl.BlockSpec(memory_space=pltpu.HBM), pl.BlockSpec(memory_space=pltpu.SMEM)],
        out_specs=[pl.BlockSpec(memory_space=pltpu.VMEM)] * len(shapes),
        out_shape=[jax.ShapeDtypeStruct((*s, 1, lanes), whole.dtype) for s in shapes],
        scratch_shapes=[pltpu.SemaphoreType.DMA((len(parts), max(len(p) for p in parts)))],
        compiler_params=pltpu.CompilerParams(vmem_limit_bytes=limit * 2**20),
        cost_estimate=pl.CostEstimate(flops=20_000_000, bytes_accessed=2**22, transcendentals=0),
        name="take",
    )(whole, low_row)
    return [g.reshape(*s, lanes) for g, s in zip(got, shapes)]


def split_body(zs, whole, *outs):
    width = outs[0].shape[1]

    @pl.loop(0, ROWS)
    def _(r):
        for z, out in zip(zs, outs):
            out[r] = whole[r, pl.ds(z, width, stride=4), :]


def split(whole, zs):
    depth, wide, lanes = whole.shape
    width = wide // 4
    return pl.pallas_call(
        lambda *refs: split_body(zs, *refs),
        grid=(depth // ROWS,),
        in_specs=[pl.BlockSpec((ROWS, wide, lanes), lambda i: (i, 0, 0))],
        out_specs=[pl.BlockSpec((ROWS, width, lanes), lambda i: (i, 0, 0))] * len(zs),
        out_shape=[jax.ShapeDtypeStruct((depth, width, lanes), whole.dtype)] * len(zs),
        compiler_params=pltpu.CompilerParams(vmem_limit_bytes=9 * 2**20),
        cost_estimate=pl.CostEstimate(flops=20_000_000, bytes_accessed=2**24, transcendentals=0),
        name="split",
    )(whole)


def face_of(z, rows):
    cuts = list(range(0, rows, 4)) + [rows]

    def piece(start, size):
        return (lambda w, low: w.at[pl.ds(low + start, size), :, z], lambda o: o.at[pl.ds(start, size)])

    return [piece(start, stop - start) for start, stop in zip(cuts, cuts[1:])]


def edge_of(pick):
    return [(lambda w, low, z=z: pick(w, z), lambda o, z=z: o.at[z]) for z in range(4)]


def halo_row(pieces, edge, low_row, depth, g):
    at = g - low_row
    row, start = None, 0
    for piece in pieces:
        rows = piece.shape[0]
        here = piece[jnp.clip(at - start, 0, rows - 1)]
        row = here if row is None else jnp.where(at < start, row, here)
        start += rows
    return jnp.where(g == (depth - 1) * (1 - low_row), edge, row)


def grow_body(plan, last, *refs):
    zs, n_in, base, depth = plan["zs"], plan["n_in"], plan["base"], plan["depth"]
    ins, outs = refs[:n_in], refs[n_in:]
    i = pl.program_id(0)
    n = pl.num_programs(0)
    width = outs[0].shape[1]
    place = lax.broadcasted_iota(jnp.int32, outs[0].shape[1:], 0)
    for j, z in enumerate(zs):
        c, before, after, d, f, south, north, west, east = (ins[a] for a in plan[z])
        low, high = ([ins[a] for a in plan[side, z]] for side in ("low", "high"))
        rest = outs[len(zs) :]

        @pl.loop(0, BAND, unroll=4 if last else 2)
        def _(r, c=c, low=low, high=high, before=before, after=after, d=d, f=f, south=south, north=north, west=west, east=east, j=j):
            x = c[r]
            edge_low = jnp.where(i == 0, south[0], before[0])
            edge_high = jnp.where(i == n - 1, north[0], after[0])
            lat_low = jnp.where(r == 0, edge_low, c[jnp.maximum(r - 1, 0)])
            lat_high = jnp.where(r == BAND - 1, edge_high, c[jnp.minimum(r + 1, BAND - 1)])
            left = jnp.where(place == 0, west[0, pl.ds(i * BAND + r, 1), :], pltpu.roll(x, 1, 0))
            right = jnp.where(place == width - 1, east[0, pl.ds(i * BAND + r, 1), :], pltpu.roll(x, width - 1, 0))
            below, above = (
                halo_row(h[:1], h[1][0], ins[0][0], depth, i * BAND + r) if len(h) == 2 else h[0][r] for h in (low, high)
            )
            spread = lat_low + lat_high + left + right + below + above - 6.0 * x
            y = x + d[r] * spread + f[r]
            outs[j][r] = y
            if last:
                total = jnp.sum(y, axis=0, keepdims=True)
                away = y - total * (1.0 / width)
                rest[0][2 * j, pl.ds(i * BAND + r, 1), :] = total
                rest[0][2 * j + 1, pl.ds(i * BAND + r, 1), :] = jnp.sum(away * away, axis=0, keepdims=True)
            else:
                rest[2][base + j, pl.ds(i * BAND + r, 1), :] = y[width - 1 :, :]
                rest[3][base + j, pl.ds(i * BAND + r, 1), :] = y[:1, :]

        if not last:

            @pl.when(i == 0)
            def _(j=j):
                rest[1][base + j] = outs[j][0]

            @pl.when(i == n - 1)
            def _(j=j):
                rest[0][base + j] = outs[j][BAND - 1]

    if plan["carried"]:
        held = [ins[a] for a in plan["carried"]]

        @pl.when(i == 0)
        def _():
            for k in range(4):
                rest[k][:base] = held[k][...]


def grow(zs, low_row, u, low, high, d, f, where, last, carried=()):
    depth, width, lanes = u[0].shape
    block = pl.BlockSpec((BAND, width, lanes), lambda i: (i, 0, 0))
    row_before = pl.BlockSpec((1, width, lanes), lambda i: (jnp.maximum(i * BAND - 1, 0), 0, 0))
    row_after = pl.BlockSpec((1, width, lanes), lambda i: (jnp.minimum(i * BAND + BAND, depth - 1), 0, 0))
    whole_face = pl.BlockSpec((depth - 1, width, lanes), lambda i: (0, 0, 0))
    whole_row = pl.BlockSpec((1, width, lanes), lambda i: (0, 0, 0))
    arrays, specs, seen = [low_row], [pl.BlockSpec(memory_space=pltpu.SMEM)], {}

    def use(key, array, spec):
        if key not in seen:
            seen[key] = len(arrays)
            arrays.append(array)
            specs.append(spec)
        return seen[key]

    plan = {"zs": zs, "depth": depth}
    for z in zs:
        sides, k = where[z]
        lat_edge = pl.BlockSpec((1, width, lanes), lambda i, k=k: (k, 0, 0))
        lon_edge = pl.BlockSpec((1, depth, lanes), lambda i, k=k: (k, 0, 0))
        plan[z] = [
            use(("u", z), u[z], block),
            use(("before", z), u[z], row_before),
            use(("after", z), u[z], row_after),
            use(("d", z), d[z], block),
            use(("f", z), f[z], block),
            use(("s", z), sides[0], lat_edge),
            use(("n", z), sides[1], lat_edge),
            use(("w", z), sides[2], lon_edge),
            use(("e", z), sides[3], lon_edge),
        ]
    for z in zs:
        for side, outer, halo, other in (("low", 0, low, z - 1), ("high", 3, high, z + 1)):
            if z == outer:
                plan[side, z] = [use((side, 0), halo[0], whole_face), use((side, 1), halo[1], whole_row)]
            else:
                plan[side, z] = [use(("u", other), u[other], block)]
    m = len(zs)
    base = carried[0].shape[0] if carried else 0
    lat_all = pl.BlockSpec((base, width, lanes), lambda i: (0, 0, 0))
    lon_all = pl.BlockSpec((base, depth, lanes), lambda i: (0, 0, 0))
    plan["carried"] = [
        use(("carried", k), a, spec) for k, (a, spec) in enumerate(zip(carried, (lat_all, lat_all, lon_all, lon_all)))
    ]
    plan["base"], plan["n_in"] = base, len(arrays)
    shapes, outs = [u[0].shape] * m, [block] * m
    if last:
        shapes += [(2 * m, depth, lanes)]
        outs += [pl.BlockSpec((2 * m, depth, lanes), lambda i: (0, 0, 0))]
    else:
        t = base + m
        shapes += [(t, width, lanes)] * 2 + [(t, depth, lanes)] * 2
        outs += [pl.BlockSpec((t, width, lanes), lambda i: (0, 0, 0))] * 2
        outs += [pl.BlockSpec((t, depth, lanes), lambda i: (0, 0, 0))] * 2
    got = pl.pallas_call(
        lambda *refs: grow_body(plan, last, *refs),
        grid=(depth // BAND,),
        in_specs=specs,
        out_specs=outs,
        out_shape=[jax.ShapeDtypeStruct(s, u[0].dtype) for s in shapes],
        compiler_params=pltpu.CompilerParams(vmem_limit_bytes=(8 if m == 1 else 13) * 2**20),
        cost_estimate=pl.CostEstimate(flops=10_000_000 * m, bytes_accessed=2**22 * m, transcendentals=0),
        name="grow",
    )(*arrays)
    return got[:m], got[m:]


def exchange(south, north, east, west):
    return (
        shift(south, "lat", 1),
        shift(north, "lat", -1),
        shift(east, "lon", 1),
        shift(west, "lon", -1),
    )


def scale_of(count, width, own, others, k):
    sums = [s[2 * k] for s in (own, *others)]
    powers = [s[2 * k + 1] for s in (own, *others)]
    mean = (sums[0] + sums[1] + sums[2] + sums[3]) * (1.0 / count)
    power = powers[0] + powers[1] + powers[2] + powers[3]
    for s in sums:
        gap = s * (1.0 / width) - mean
        power = power + width * (gap * gap)
    return mean, lax.rsqrt(power * (1.0 / count) + 0.0001)


def finish_body(count, zs, *refs):
    m = len(zs)
    planes, stats, (score, end) = refs[:m], refs[m:-2], refs[-2:]
    width = planes[0].shape[1]
    for k, z in enumerate(zs):
        mean, scale = scale_of(count, width, stats[0], stats[1:], k)
        for r in range(ROWS):
            y = planes[k][r]
            end[r, pl.ds(z, width, stride=4), :] = y
            score[r, pl.ds(z, width, stride=4), :] = (y - mean[r : r + 1, :]) * scale[r : r + 1, :]


def finish(zs, planes, stats):
    depth, width, lanes = planes[0].shape
    m = len(zs)
    block = pl.BlockSpec((ROWS, width, lanes), lambda i: (i, 0, 0))
    wide = pl.BlockSpec((ROWS, 4 * width, lanes), lambda i: (i, 0, 0))
    stat = pl.BlockSpec((2 * m, ROWS, lanes), lambda i: (0, i, 0))
    count = width * lax.axis_size("lon")
    full = jax.ShapeDtypeStruct((depth, 4 * width, lanes), planes[0].dtype)
    return pl.pallas_call(
        lambda *refs: finish_body(count, zs, *refs),
        grid=(depth // ROWS,),
        in_specs=[block] * m + [stat] * 4,
        out_specs=[wide] * 2,
        out_shape=[full] * 2,
        compiler_params=pltpu.CompilerParams(vmem_limit_bytes=24 * 2**20),
        cost_estimate=pl.CostEstimate(flops=30_000_000, bytes_accessed=2**24, transcendentals=0),
        name="finish",
    )(*planes, *stats)


def put_body(start, _, source, out, sems):
    copies = [
        pltpu.make_async_copy(
            source.at[pl.ds(k * ROWS, ROWS)], out.at[pl.ds(start + k * ROWS, ROWS), :, 0], sems.at[k]
        )
        for k in range(source.shape[0] // ROWS)
    ]
    for copy in copies:
        copy.start()
    for copy in copies:
        copy.wait()


def put(view, rows, start):
    depth, width, lanes = rows.shape
    return pl.pallas_call(
        lambda *refs: put_body(start, *refs),
        in_specs=[pl.BlockSpec(memory_space=pltpu.HBM), pl.BlockSpec(memory_space=pltpu.VMEM)],
        out_specs=pl.BlockSpec(memory_space=pltpu.HBM),
        out_shape=jax.ShapeDtypeStruct(view.shape, view.dtype),
        scratch_shapes=[pltpu.SemaphoreType.DMA((depth // ROWS,))],
        input_output_aliases={0: 0},
        compiler_params=pltpu.CompilerParams(vmem_limit_bytes=2**20),
        cost_estimate=pl.CostEstimate(flops=5_000_000, bytes_accessed=2**21, transcendentals=0),
        name="put",
    )(view, rows.reshape(depth, width, 1, lanes))


def put_scaled_body(count, start, _, plane, own, s1, s2, s3, out, held, sems):
    depth, width, _ = plane.shape
    mean, scale = scale_of(count, width, own, (s1, s2, s3), 0)
    copies = []
    for k in range(depth // ROWS):
        for r in range(k * ROWS, (k + 1) * ROWS):
            held[r, :, 0, :] = (plane[r] - mean[r : r + 1, :]) * scale[r : r + 1, :]
        copies.append(
            pltpu.make_async_copy(
                held.at[pl.ds(k * ROWS, ROWS)], out.at[pl.ds(start + k * ROWS, ROWS), :, 0], sems.at[k]
            )
        )
        copies[-1].start()
    for copy in copies:
        copy.wait()


def put_scaled(view, rows, stats, start):
    depth, width, lanes = rows.shape
    count = width * lax.axis_size("lon")
    return pl.pallas_call(
        lambda *refs: put_scaled_body(count, start, *refs),
        in_specs=[pl.BlockSpec(memory_space=pltpu.HBM)] + [pl.BlockSpec(memory_space=pltpu.VMEM)] * 5,
        out_specs=pl.BlockSpec(memory_space=pltpu.HBM),
        out_shape=jax.ShapeDtypeStruct(view.shape, view.dtype),
        scratch_shapes=[
            pltpu.VMEM((depth, width, 1, lanes), rows.dtype),
            pltpu.SemaphoreType.DMA((depth // ROWS,)),
        ],
        input_output_aliases={0: 0},
        compiler_params=pltpu.CompilerParams(vmem_limit_bytes=4 * 2**20),
        cost_estimate=pl.CostEstimate(flops=5_000_000, bytes_accessed=2**21, transcendentals=0),
        name="put_scaled",
    )(view, rows, *stats)


def grow_last_body(start, k, low_row, c, high, d, f, south, north, west, east, edge, *refs):
    pieces, (out, stat) = refs[:-2], refs[-2:]
    depth, width, _ = c.shape
    rows = out.shape[0]
    place = lax.broadcasted_iota(jnp.int32, c.shape[1:], 0)

    @pl.loop(0, rows, unroll=2)
    def _(i):
        r = start + i
        x = c[r]
        lat_low = jnp.where(r == 0, south[k], c[jnp.maximum(r - 1, 0)])
        lat_high = jnp.where(r == depth - 1, north[k], c[jnp.minimum(r + 1, depth - 1)])
        left = jnp.where(place == 0, west[k, pl.ds(r, 1), :], pltpu.roll(x, 1, 0))
        right = jnp.where(place == width - 1, east[k, pl.ds(r, 1), :], pltpu.roll(x, width - 1, 0))
        below = halo_row(pieces, edge[0], low_row[0], depth, r)
        spread = lat_low + lat_high + left + right + below + high[r] - 6.0 * x
        y = x + d[r] * spread + f[r]
        out[i] = y
        total = jnp.sum(y, axis=0, keepdims=True)
        away = y - total * (1.0 / width)
        stat[0, pl.ds(i, 1), :] = total
        stat[1, pl.ds(i, 1), :] = jnp.sum(away * away, axis=0, keepdims=True)


def grow_last(start, rows, low_row, u, pieces, edge, d, f, where):
    sides, k = where
    _, width, lanes = u[0].shape
    vmem = pl.BlockSpec(memory_space=pltpu.VMEM)
    return pl.pallas_call(
        lambda *refs: grow_last_body(start, k, *refs),
        in_specs=[pl.BlockSpec(memory_space=pltpu.SMEM)] + [vmem] * (9 + len(pieces)),
        out_specs=[vmem] * 2,
        out_shape=[
            jax.ShapeDtypeStruct((rows, width, lanes), u[0].dtype),
            jax.ShapeDtypeStruct((2, rows, lanes), u[0].dtype),
        ],
        compiler_params=pltpu.CompilerParams(vmem_limit_bytes=2**20),
        cost_estimate=pl.CostEstimate(flops=10_000_000, bytes_accessed=2**22, transcendentals=0),
        name="grow_last",
    )(low_row, u[0], u[1], d, f, *sides, edge, *pieces)


def from_all(x):
    return [x] + [shift(x, "lon", by) for by in (1, -1, 2)]


def local_call(body, shapes, low_row, *arrays):
    vmem = pl.BlockSpec(memory_space=pltpu.VMEM)
    return pl.pallas_call(
        body,
        in_specs=[pl.BlockSpec(memory_space=pltpu.SMEM)] + [vmem] * len(arrays),
        out_specs=[vmem] * len(shapes),
        out_shape=[jax.ShapeDtypeStruct(s, arrays[0].dtype) for s in shapes],
        compiler_params=pltpu.CompilerParams(vmem_limit_bytes=2**20),
        cost_estimate=pl.CostEstimate(flops=2_000_000, bytes_accessed=2**21, transcendentals=0),
    )(low_row, *arrays)


def pick(sides, places, low_row):
    def body(low, south, north, *outs):
        for place, out in zip(places, outs):
            out[0] = jnp.where(low[0] == 1, south[place], north[place])

    return local_call(body, [(1, *sides[0].shape[1:])] * len(places), low_row, *sides[:2])


def cut(plane, start, rows, low_row):
    def body(low, whole, out):
        @pl.loop(0, rows)
        def _(r):
            out[r] = whole[low[0] + start + r]

    return local_call(body, [(rows, *plane.shape[1:])], low_row, plane)[0]


def relay(row, by):
    lat, lev = lax.axis_size("lat"), lax.axis_size("lev")
    pairs = []
    for a in range(lat):
        for b in range(lev):
            to = (a + (1 if a % 2 else -1)) % lat, (b + by) % lev
            pairs.append((a * lev + b, to[0] * lev + to[1]))
    return lax.ppermute(row, ("lat", "lev"), pairs)


def local(initial_heat, diffusivity_ratio, forcing_term):
    depth, width, _, lanes = initial_heat.shape
    face = (depth - 1, width)
    view = initial_heat.reshape(depth, width, 4, 1, lanes)
    raw, d, f = (a.reshape(depth, 4 * width, lanes) for a in (initial_heat, diffusivity_ratio, forcing_term))
    low_start = 1 - lax.axis_index("lat") % 2
    low_row = jnp.full((1,), low_start, jnp.int32)
    (send,) = take(view, low_row, [face], [face_of(3, depth - 1)], 50)
    up = shift(send, "lev", 1)
    send, *rest = take(
        view,
        low_row,
        [face, (4, width), (4, width), (4, depth), (4, depth)],
        [
            face_of(0, depth - 1),
            edge_of(lambda w, z: w.at[depth - 1, :, z]),
            edge_of(lambda w, z: w.at[0, :, z]),
            edge_of(lambda w, z: w.at[:, width - 1, z]),
            edge_of(lambda w, z: w.at[:, 0, z]),
        ],
        50,
    )
    sides = exchange(*rest)
    down = shift(send, "lev", -1)
    u, d, f = (split(a, (0, 1, 2, 3)) for a in (raw, d, f))
    order = (0, 1, 2, 3)
    for step in range(STEPS):
        where = [(sides, order.index(z)) for z in range(4)]
        rows = pick(sides, (order.index(3), order.index(0)), low_row)
        low, high = (up, relay(rows[0], 1)), (down, relay(rows[1], -1))
        if step == STEPS - 1:
            break
        first, second = (0, 3) if step % 2 == 0 else (3, 0)
        most = (first, 1, 2) if first == 0 else (3, 2, 1)
        made, carried = grow(most, low_row, u, low, high, d, f, where, False)
        early = shift(cut(made[0], 0, depth - 1, low_row), "lev", -1 if first == 0 else 1)
        (v,), rest = grow((second,), low_row, u, low, high, d, f, where, False, carried)
        sides = exchange(*rest)
        if step < STEPS - 2:
            late = shift(cut(v, 0, depth - 1, low_row), "lev", -1 if second == 0 else 1)
        else:
            late = [shift(cut(v, 0, CUT, low_row), "lev", 1)]
            late.append(shift(cut(v, CUT, depth - 1 - CUT, low_row), "lev", 1))
        order = most + (second,)
        made = dict(zip(order, [*made, v]))
        u = [made[z] for z in range(4)]
        up, down = (late, early) if first == 0 else (early, late)
    made, (stat,) = grow((3, 2, 1), low_row, u, low, high, d, f, where, True)
    stats = from_all(stat)
    filled = finish((3, 2, 1), made, stats)
    score, end = (x.reshape(depth, width, 4, 1, lanes) for x in filled)
    pieces, edge = low
    for name, start, stop in (("b", 0, CUT), ("c", CUT, depth)):
        near = pieces[:1] if name == "b" else pieces
        rows, stat = grow_last(start, stop - start, low_row, u, near, edge, d[0], f[0], where[0])
        stats = from_all(stat)
        end = put(end, rows, start)
        score = put_scaled(score, rows, stats, start)
    return score.reshape(initial_heat.shape), end.reshape(initial_heat.shape)


def solution(mesh):
    placed = P("lat", "lon", "lev", None)

    return jax.shard_map(
        local,
        mesh=mesh,
        in_specs=(placed,) * 3,
        out_specs=(placed, placed),
        check_vma=False,
    )
```

profile of v0, /device:TPU:1, one launch (start us, length us, event | category | flops | bytes accessed | tf_op | source)
XLA Modules:
  0.0 477.6 jit_solution(12948088565846591149)
XLA Ops:
  0.6 2.8 take.3
  3.5 2.1 collective-permute-start.6
  5.6 3.3 take.2
  8.9 2.5 collective-permute-start.4
  12.5 2.7 collective-permute-start
  15.2 1.6 collective-permute-start.2
  16.9 85.0 %collective-permute-done.1.north.refs_7_.refs_16_.refs_25_ = f32[4,128,128]{2,1,0:T(8,128)S(1)} collective-permute-done((f32[4,128,128]{2,1,0:T(8,128)S(1)}, f32[4,128,128]{2,1,0:T(8,128)S(1)}, u32[]{:S(2)}, u32[]{:S(2)}) %collective-permute-start.1) | collective-permute-done | bytes 262176 | tf_op jit(solution)/shard_map/ppermute | solution.py:17
  101.9 3.8 collective-permute-start.3
  106.2 3.4 copy-done
  110.4 3.7 copy-done.1
  114.8 1.5 slice-done.1
  117.1 6.8 %grow.7 = (f32[32,128,128]{2,1,0:T(8,128)S(1)}, f32[32,128,128]{2,1,0:T(8,128)S(1)}, f32[32,128,128]{2,1,0:T(8,128)S(1)}, f32[3,128,128]{2,1,0:T(8,128)S(1)}, f3...) custom-call(s32[1]{0:T(128)} %bitcast.refs_1_.low.refs_0_, ...), custom_call_target="tpu_custom_call" | custom-call | flops 30000000 | bytes 12582912 | tf_op jit(solution)/shard_map/grow/pallas_call | solution.py:207
  124.2 1.6 collective-permute-start.12
  125.8 3.1 collective-permute-start.5
  128.9 2.6 collective-permute-done.5.refs_12_
  132.8 1.6 copy-done.3
  134.4 1.8 grow.8
  136.5 1.7 collective-permute-start.14
  138.2 2.7 collective-permute-start.8
  140.9 78.4 %collective-permute-done.8.south.refs_6_.refs_15_.refs_24_ = f32[4,128,128]{2,1,0:T(8,128)S(1)} collective-permute-done((f32[4,128,128]{2,1,0:T(8,128)S(1)}, f32[4,128,128]{2,1,0:T(8,128)S(1)}, u32[]{:S(2)}, u32[]{:S(2)}) %collective-permute-start.8) | collective-permute-done | bytes 262176 | tf_op jit(solution)/shard_map/ppermute | solution.py:17
  219.4 3.0 collective-permute-done.9.north.refs_7_.refs_16_.refs_25_
  222.4 1.6 collective-permute-start.13
  224.0 3.9 collective-permute-done.13.refs_29_
  227.9 4.7 grow.9
  233.0 8.6 %collective-permute-done.15.refs_11_ = f32[1,128,128]{2,1,0:T(8,128)S(1)} collective-permute-done((f32[1,128,128]{2,1,0:T(8,128)S(1)}, f32[1,128,128]{2,1,0:T(8,128)S(1)}, u32[]{:S(2)}, u32[]{:S(2)}) %collective-permute-start.15) | collective-permute-done | bytes 65568 | tf_op jit(solution)/shard_map/ppermute | solution.py:418
  241.6 1.8 grow.10
  243.8 1.5 collective-permute-start.16
  246.1 79.0 %collective-permute-done.16.south.refs_6_.refs_15_.refs_24_ = f32[4,128,128]{2,1,0:T(8,128)S(1)} collective-permute-done((f32[4,128,128]{2,1,0:T(8,128)S(1)}, f32[4,128,128]{2,1,0:T(8,128)S(1)}, u32[]{:S(2)}, u32[]{:S(2)}) %collective-permute-start.16) | collective-permute-done | bytes 262176 | tf_op jit(solution)/shard_map/ppermute | solution.py:17
  325.0 2.2 collective-permute-start.19
  328.2 5.5 %collective-permute-start.23 = (f32[1,128,128]{2,1,0:T(8,128)S(1)}, f32[1,128,128]{2,1,0:T(8,128)S(1)}, u32[]{:S(2)}, u32[]{:S(2)}) collective-permute-start(f32[1,128,128]{2,1,0:T(8,128)S(1)} %get-tuple-element.119), channel_id=1, source_target_pairs={{0,97},{1,98},{2,99},{3,100},{4,101},{5,102},{6,103},{7,96},{32,65... | collective-permute-start | bytes 196616 | tf_op jit(solution)/shard_map/ppermute | solution.py:418
  333.7 4.3 collective-permute-done.23.refs_29_
  337.9 5.0 %grow.11 = (f32[32,128,128]{2,1,0:T(8,128)S(1)}, f32[32,128,128]{2,1,0:T(8,128)S(1)}, f32[32,128,128]{2,1,0:T(8,128)S(1)}, f32[3,128,128]{2,1,0:T(8,128)S(1)}, f...) custom-call(s32[1]{0:T(128)} %bitcast.refs_1_.low.refs_0_, ...), custom_call_target="tpu_custom_call" | custom-call | flops 30000000 | bytes 12582912 | tf_op jit(solution)/shard_map/grow/pallas_call | solution.py:207
  343.3 3.0 collective-permute-start.21
  346.4 2.0 collective-permute-done.21.refs_12_
  348.3 2.0 grow.12
  350.5 2.1 collective-permute-start.34
  352.8 2.1 collective-permute-start.24
  355.0 81.9 %collective-permute-done.24.south.refs_6_.refs_15_.refs_24_.refs_5_ = f32[4,128,128]{2,1,0:T(8,128)S(1)} collective-permute-done((f32[4,128,128]{2,1,0:T(8,128)S(1)}, f32[4,128,128]{2,1,0:T(8,128)S(1)}, u32[]{:S(2)}, u32[]{:S(2)}) %collective-permute-start.24) | collective-permute-done | bytes 262176 | tf_op jit(solution)/shard_map/ppermute | solution.py:17
  436.9 3.5 collective-permute-done.25.north.refs_7_.refs_16_.refs_25_.refs_6_
  440.4 2.4 collective-permute-start.27
  442.8 3.9 collective-permute-start.29
  446.7 1.3 collective-permute-done.29.refs_29_
  448.0 4.6 grow.13
  455.4 3.0 collective-permute-start.37
  461.9 2.8 collective-permute-start.41
  466.2 6.3 %finish.1 = (f32[32,512,128]{2,1,0:T(8,128)}, f32[32,512,128]{2,1,0:T(8,128)}) custom-call(f32[32,128,128]{2,1,0:T(8,128)S(1)} %get-tuple-element.133.refs_0_, f32[32,128,128]{2,1,0:T(8,128)S(1)} %get-tuple-element.134.refs_1_, f32[32,128,128]{2,1,0:T(8,128)S(1)} %get-tuple-element.135.refs_2_, f32[6,32,128]{2,1,0:T(8,128)S(1)} %get-tuple-element.136.refs_3_, ...), custom_call_target="tpu_custom_call" | custom-call | flops 30000000 | bytes 16777216 | tf_op jit(solution)/shard_map/finish/pallas_call | solution.py:260
  474.5 1.5 put_scaled.2.refs_0_
  476.0 1.5 put_scaled.3
  (79 shorter events, 18.7 us)
Async XLA Ops:
  3.5 113.6 %collective-permute-start.6 = (f32[31,128,128]{2,1,0:T(8,128)}, f32[31,128,128]{2,1,0:T(8,128)}, u32[]{:S(2)}, u32[]{:S(2)}) collective-permute-start(f32[31,128,128]{2,1,0:T(8,128)} %bitcast.10), channel_id=1, source_target_pairs={{0,1},{1,2},{2,3},{3,4},{4,5},{5,6},{6,7},{7,0},{8,9},{9,10},{10,1... | collective-permute-start | bytes 6094856 | tf_op jit(solution)/shard_map/ppermute | solution.py:17
  8.9 122.6 %collective-permute-start.4 = (f32[31,128,128]{2,1,0:T(8,128)}, f32[31,128,128]{2,1,0:T(8,128)S(1)}, u32[]{:S(2)}, u32[]{:S(2)}) collective-permute-start(f32[31,128,128]{2,1,0:T(8,128)} %bitcast.9), channel_id=1, source_target_pairs={{0,7},{1,0},{2,1},{3,2},{4,3},{5,4},{6,5},{7,6},{8,15},{9,8},{10,9... | collective-permute-start | bytes 6094856 | tf_op jit(solution)/shard_map/ppermute | solution.py:17
  11.5 90.4 %collective-permute-start.1 = (f32[4,128,128]{2,1,0:T(8,128)S(1)}, f32[4,128,128]{2,1,0:T(8,128)S(1)}, u32[]{:S(2)}, u32[]{:S(2)}) collective-permute-start(f32[4,128,128]{2,1,0:T(8,128)S(1)} %bitcast.27), channel_id=1, source_target_pairs={{0,96},{32,0},{64,32},{96,64},{1,97},{33,1},{65,33},{97,65},{2,98}... | collective-permute-start | bytes 786440 | tf_op jit(solution)/shard_map/ppermute | solution.py:17
  12.5 93.2 %collective-permute-start = (f32[4,128,128]{2,1,0:T(8,128)S(1)}, f32[4,128,128]{2,1,0:T(8,128)S(1)}, u32[]{:S(2)}, u32[]{:S(2)}) collective-permute-start(f32[4,128,128]{2,1,0:T(8,128)S(1)} %bitcast.26), channel_id=1, source_target_pairs={{0,32},{32,64},{64,96},{96,0},{1,33},{33,65},{65,97},{97,1},{2,34}... | collective-permute-start | bytes 786440 | tf_op jit(solution)/shard_map/ppermute | solution.py:17
  15.2 101.8 %collective-permute-start.2 = (f32[4,32,128]{2,1,0:T(8,128)S(1)}, f32[4,32,128]{2,1,0:T(8,128)S(1)}, u32[]{:S(2)}, u32[]{:S(2)}) collective-permute-start(f32[4,32,128]{2,1,0:T(8,128)S(1)} %bitcast.29), channel_id=1, source_target_pairs={{0,8},{8,16},{16,24},{24,0},{1,9},{9,17},{17,25},{25,1},{2,10},{10... | collective-permute-start | bytes 196616 | tf_op jit(solution)/shard_map/ppermute | solution.py:17
  101.9 15.1 %collective-permute-start.3 = (f32[4,32,128]{2,1,0:T(8,128)S(1)}, f32[4,32,128]{2,1,0:T(8,128)S(1)}, u32[]{:S(2)}, u32[]{:S(2)}) collective-permute-start(f32[4,32,128]{2,1,0:T(8,128)S(1)} %bitcast.28), channel_id=1, source_target_pairs={{0,24},{8,0},{16,8},{24,16},{1,25},{9,1},{17,9},{25,17},{2,26},{10... | collective-permute-start | bytes 196616 | tf_op jit(solution)/shard_map/ppermute | solution.py:17
  105.7 11.4 %collective-permute-start.7 = (f32[1,128,128]{2,1,0:T(8,128)S(1)}, f32[1,128,128]{2,1,0:T(8,128)S(1)}, u32[]{:S(2)}, u32[]{:S(2)}) collective-permute-start(f32[1,128,128]{2,1,0:T(8,128)S(1)} %get-tuple-element.91), channel_id=1, source_target_pairs={{0,97},{1,98},{2,99},{3,100},{4,101},{5,102},{6,103},{7,96},{32,65... | collective-permute-start | bytes 196616 | tf_op jit(solution)/shard_map/ppermute | solution.py:418
  106.2 3.4 copy-start
  109.6 5.2 %slice-start = ((s8[8388608]{0:T(1024)(128)(4,1)}), s8[4194304]{0:T(1024)(128)(4,1)S(1)}, s32[]{:S(2)}) async-start(s8[8388608]{0:T(1024)(128)(4,1)} %bitcast.19), calls=%async_computation | async-start | bytes 8388608
  110.3 3.7 copy-start.1
  114.1 2.2 slice-start.1
  124.2 103.7 %collective-permute-start.12 = (f32[31,128,128]{2,1,0:T(8,128)S(1)}, f32[31,128,128]{2,1,0:T(8,128)S(1)}, u32[]{:S(2)}, u32[]{:S(2)}) collective-permute-start(f32[31,128,128]{2,1,0:T(8,128)S(1)} %shard_map.51), channel_id=1, source_target_pairs={{0,7},{1,0},{2,1},{3,2},{4,3},{5,4},{6,5},{7,6},{8,15},{9,8},{10,9... | collective-permute-start | bytes 6094856 | tf_op jit(solution)/shard_map/ppermute | solution.py:17
  125.8 5.7 %collective-permute-start.5 = (f32[1,128,128]{2,1,0:T(8,128)S(1)}, f32[1,128,128]{2,1,0:T(8,128)S(1)}, u32[]{:S(2)}, u32[]{:S(2)}) collective-permute-start(f32[1,128,128]{2,1,0:T(8,128)S(1)} %get-tuple-element.82), channel_id=1, source_target_pairs={{0,103},{1,96},{2,97},{3,98},{4,99},{5,100},{6,101},{7,102},{32,71... | collective-permute-start | bytes 196616 | tf_op jit(solution)/shard_map/ppermute | solution.py:418
  131.5 1.3 copy-start.2
  132.8 1.6 copy-start.3
  136.5 105.1 %collective-permute-start.14 = (f32[31,128,128]{2,1,0:T(8,128)S(1)}, f32[31,128,128]{2,1,0:T(8,128)S(1)}, u32[]{:S(2)}, u32[]{:S(2)}) collective-permute-start(f32[31,128,128]{2,1,0:T(8,128)S(1)} %shard_map.53), channel_id=1, source_target_pairs={{0,1},{1,2},{2,3},{3,4},{4,5},{5,6},{6,7},{7,0},{8,9},{9,10},{10,1... | collective-permute-start | bytes 6094856 | tf_op jit(solution)/shard_map/ppermute | solution.py:17
  138.2 81.1 %collective-permute-start.8 = (f32[4,128,128]{2,1,0:T(8,128)S(1)}, f32[4,128,128]{2,1,0:T(8,128)S(1)}, u32[]{:S(2)}, u32[]{:S(2)}) collective-permute-start(f32[4,128,128]{2,1,0:T(8,128)S(1)} %get-tuple-element.97), channel_id=1, source_target_pairs={{0,32},{32,64},{64,96},{96,0},{1,33},{33,65},{65,97},{97,1},{2,34}... | collective-permute-start | bytes 786440 | tf_op jit(solution)/shard_map/ppermute | solution.py:17
  140.9 81.5 %collective-permute-start.9 = (f32[4,128,128]{2,1,0:T(8,128)S(1)}, f32[4,128,128]{2,1,0:T(8,128)S(1)}, u32[]{:S(2)}, u32[]{:S(2)}) collective-permute-start(f32[4,128,128]{2,1,0:T(8,128)S(1)} %get-tuple-element.98), channel_id=1, source_target_pairs={{0,96},{32,0},{64,32},{96,64},{1,97},{33,1},{65,33},{97,65},{2,98}... | collective-permute-start | bytes 786440 | tf_op jit(solution)/shard_map/ppermute | solution.py:17
  140.9 83.1 %collective-permute-start.10 = (f32[4,32,128]{2,1,0:T(8,128)S(1)}, f32[4,32,128]{2,1,0:T(8,128)S(1)}, u32[]{:S(2)}, u32[]{:S(2)}) collective-permute-start(f32[4,32,128]{2,1,0:T(8,128)S(1)} %get-tuple-element.99), channel_id=1, source_target_pairs={{0,8},{8,16},{16,24},{24,0},{1,9},{9,17},{17,25},{25,1},{2,10},{10... | collective-permute-start | bytes 196616 | tf_op jit(solution)/shard_map/ppermute | solution.py:17
  219.3 4.7 collective-permute-start.11
  222.4 5.5 %collective-permute-start.13 = (f32[1,128,128]{2,1,0:T(8,128)S(1)}, f32[1,128,128]{2,1,0:T(8,128)S(1)}, u32[]{:S(2)}, u32[]{:S(2)}) collective-permute-start(f32[1,128,128]{2,1,0:T(8,128)S(1)} %get-tuple-element.104), channel_id=1, source_target_pairs={{0,103},{1,96},{2,97},{3,98},{4,99},{5,100},{6,101},{7,102},{32,71... | collective-permute-start | bytes 196616 | tf_op jit(solution)/shard_map/ppermute | solution.py:418
  232.8 105.1 %collective-permute-start.22 = (f32[31,128,128]{2,1,0:T(8,128)S(1)}, f32[31,128,128]{2,1,0:T(8,128)S(1)}, u32[]{:S(2)}, u32[]{:S(2)}) collective-permute-start(f32[31,128,128]{2,1,0:T(8,128)S(1)} %shard_map.56), channel_id=1, source_target_pairs={{0,1},{1,2},{2,3},{3,4},{4,5},{5,6},{6,7},{7,0},{8,9},{9,10},{10,1... | collective-permute-start | bytes 6094856 | tf_op jit(solution)/shard_map/ppermute | solution.py:17
  232.9 8.7 %collective-permute-start.15 = (f32[1,128,128]{2,1,0:T(8,128)S(1)}, f32[1,128,128]{2,1,0:T(8,128)S(1)}, u32[]{:S(2)}, u32[]{:S(2)}) collective-permute-start(f32[1,128,128]{2,1,0:T(8,128)S(1)} %get-tuple-element.106), channel_id=1, source_target_pairs={{0,97},{1,98},{2,99},{3,100},{4,101},{5,102},{6,103},{7,96},{32,65... | collective-permute-start | bytes 196616 | tf_op jit(solution)/shard_map/ppermute | solution.py:418
  243.7 104.6 %collective-permute-start.20 = (f32[31,128,128]{2,1,0:T(8,128)S(1)}, f32[31,128,128]{2,1,0:T(8,128)S(1)}, u32[]{:S(2)}, u32[]{:S(2)}) collective-permute-start(f32[31,128,128]{2,1,0:T(8,128)S(1)} %shard_map.54), channel_id=1, source_target_pairs={{0,7},{1,0},{2,1},{3,2},{4,3},{5,4},{6,5},{7,6},{8,15},{9,8},{10,9... | collective-permute-start | bytes 6094856 | tf_op jit(solution)/shard_map/ppermute | solution.py:17
  243.8 81.2 %collective-permute-start.16 = (f32[4,128,128]{2,1,0:T(8,128)S(1)}, f32[4,128,128]{2,1,0:T(8,128)S(1)}, u32[]{:S(2)}, u32[]{:S(2)}) collective-permute-start(f32[4,128,128]{2,1,0:T(8,128)S(1)} %get-tuple-element.111), channel_id=1, source_target_pairs={{0,32},{32,64},{64,96},{96,0},{1,33},{33,65},{65,97},{97,1},{2,34}... | collective-permute-start | bytes 786440 | tf_op jit(solution)/shard_map/ppermute | solution.py:17
  245.3 82.8 %collective-permute-start.17 = (f32[4,128,128]{2,1,0:T(8,128)S(1)}, f32[4,128,128]{2,1,0:T(8,128)S(1)}, u32[]{:S(2)}, u32[]{:S(2)}) collective-permute-start(f32[4,128,128]{2,1,0:T(8,128)S(1)} %get-tuple-element.112), channel_id=1, source_target_pairs={{0,96},{32,0},{64,32},{96,64},{1,97},{33,1},{65,33},{97,65},{2,98}... | collective-permute-start | bytes 786440 | tf_op jit(solution)/shard_map/ppermute | solution.py:17
  245.3 88.3 %collective-permute-start.18 = (f32[4,32,128]{2,1,0:T(8,128)S(1)}, f32[4,32,128]{2,1,0:T(8,128)S(1)}, u32[]{:S(2)}, u32[]{:S(2)}) collective-permute-start(f32[4,32,128]{2,1,0:T(8,128)S(1)} %get-tuple-element.113), channel_id=1, source_target_pairs={{0,8},{8,16},{16,24},{24,0},{1,9},{9,17},{17,25},{25,1},{2,10},{10... | collective-permute-start | bytes 196616 | tf_op jit(solution)/shard_map/ppermute | solution.py:17
  325.0 8.6 %collective-permute-start.19 = (f32[4,32,128]{2,1,0:T(8,128)S(1)}, f32[4,32,128]{2,1,0:T(8,128)S(1)}, u32[]{:S(2)}, u32[]{:S(2)}) collective-permute-start(f32[4,32,128]{2,1,0:T(8,128)S(1)} %get-tuple-element.114), channel_id=1, source_target_pairs={{0,24},{8,0},{16,8},{24,16},{1,25},{9,1},{17,9},{25,17},{2,26},{10... | collective-permute-start | bytes 196616 | tf_op jit(solution)/shard_map/ppermute | solution.py:17
  328.2 9.8 %collective-permute-start.23 = (f32[1,128,128]{2,1,0:T(8,128)S(1)}, f32[1,128,128]{2,1,0:T(8,128)S(1)}, u32[]{:S(2)}, u32[]{:S(2)}) collective-permute-start(f32[1,128,128]{2,1,0:T(8,128)S(1)} %get-tuple-element.119), channel_id=1, source_target_pairs={{0,97},{1,98},{2,99},{3,100},{4,101},{5,102},{6,103},{7,96},{32,65... | collective-permute-start | bytes 196616 | tf_op jit(solution)/shard_map/ppermute | solution.py:418
  343.3 104.8 %collective-permute-start.28 = (f32[31,128,128]{2,1,0:T(8,128)S(1)}, f32[31,128,128]{2,1,0:T(8,128)S(1)}, u32[]{:S(2)}, u32[]{:S(2)}) collective-permute-start(f32[31,128,128]{2,1,0:T(8,128)S(1)} %shard_map.57), channel_id=1, source_target_pairs={{0,7},{1,0},{2,1},{3,2},{4,3},{5,4},{6,5},{7,6},{8,15},{9,8},{10,9... | collective-permute-start | bytes 6094856 | tf_op jit(solution)/shard_map/ppermute | solution.py:17
  343.3 5.0 %collective-permute-start.21 = (f32[1,128,128]{2,1,0:T(8,128)S(1)}, f32[1,128,128]{2,1,0:T(8,128)S(1)}, u32[]{:S(2)}, u32[]{:S(2)}) collective-permute-start(f32[1,128,128]{2,1,0:T(8,128)S(1)} %get-tuple-element.117), channel_id=1, source_target_pairs={{0,103},{1,96},{2,97},{3,98},{4,99},{5,100},{6,101},{7,102},{32,71... | collective-permute-start | bytes 196616 | tf_op jit(solution)/shard_map/ppermute | solution.py:418
  350.5 103.8 %collective-permute-start.34 = (f32[16,128,128]{2,1,0:T(8,128)S(1)}, f32[16,128,128]{2,1,0:T(8,128)S(1)}, u32[]{:S(2)}, u32[]{:S(2)}) collective-permute-start(f32[16,128,128]{2,1,0:T(8,128)S(1)} %shard_map.59), channel_id=1, source_target_pairs={{0,1},{1,2},{2,3},{3,4},{4,5},{5,6},{6,7},{7,0},{8,9},{9,10},{10,1... | collective-permute-start | bytes 3145736 | tf_op jit(solution)/shard_map/ppermute | solution.py:17
  352.7 105.6 %collective-permute-start.38 = (f32[15,128,128]{2,1,0:T(8,128)S(1)}, f32[15,128,128]{2,1,0:T(8,128)S(1)}, u32[]{:S(2)}, u32[]{:S(2)}) collective-permute-start(f32[15,128,128]{2,1,0:T(8,128)S(1)} %shard_map.60), channel_id=1, source_target_pairs={{0,1},{1,2},{2,3},{3,4},{4,5},{5,6},{6,7},{7,0},{8,9},{9,10},{10,1... | collective-permute-start | bytes 2949128 | tf_op jit(solution)/shard_map/ppermute | solution.py:17
  352.8 84.1 %collective-permute-start.24 = (f32[4,128,128]{2,1,0:T(8,128)S(1)}, f32[4,128,128]{2,1,0:T(8,128)S(1)}, u32[]{:S(2)}, u32[]{:S(2)}) collective-permute-start(f32[4,128,128]{2,1,0:T(8,128)S(1)} %get-tuple-element.125), channel_id=1, source_target_pairs={{0,32},{32,64},{64,96},{96,0},{1,33},{33,65},{65,97},{97,1},{2,34}... | collective-permute-start | bytes 786440 | tf_op jit(solution)/shard_map/ppermute | solution.py:17
  355.0 85.5 %collective-permute-start.25 = (f32[4,128,128]{2,1,0:T(8,128)S(1)}, f32[4,128,128]{2,1,0:T(8,128)S(1)}, u32[]{:S(2)}, u32[]{:S(2)}) collective-permute-start(f32[4,128,128]{2,1,0:T(8,128)S(1)} %get-tuple-element.126), channel_id=1, source_target_pairs={{0,96},{32,0},{64,32},{96,64},{1,97},{33,1},{65,33},{97,65},{2,98}... | collective-permute-start | bytes 786440 | tf_op jit(solution)/shard_map/ppermute | solution.py:17
  436.9 5.9 %collective-permute-start.26 = (f32[4,32,128]{2,1,0:T(8,128)S(1)}, f32[4,32,128]{2,1,0:T(8,128)S(1)}, u32[]{:S(2)}, u32[]{:S(2)}) collective-permute-start(f32[4,32,128]{2,1,0:T(8,128)S(1)} %get-tuple-element.127), channel_id=1, source_target_pairs={{0,8},{8,16},{16,24},{24,0},{1,9},{9,17},{17,25},{25,1},{2,10},{10... | collective-permute-start | bytes 196616 | tf_op jit(solution)/shard_map/ppermute | solution.py:17
  440.4 6.3 %collective-permute-start.27 = (f32[4,32,128]{2,1,0:T(8,128)S(1)}, f32[4,32,128]{2,1,0:T(8,128)S(1)}, u32[]{:S(2)}, u32[]{:S(2)}) collective-permute-start(f32[4,32,128]{2,1,0:T(8,128)S(1)} %get-tuple-element.128), channel_id=1, source_target_pairs={{0,24},{8,0},{16,8},{24,16},{1,25},{9,1},{17,9},{25,17},{2,26},{10... | collective-permute-start | bytes 196616 | tf_op jit(solution)/shard_map/ppermute | solution.py:17
  442.8 5.2 %collective-permute-start.29 = (f32[1,128,128]{2,1,0:T(8,128)S(1)}, f32[1,128,128]{2,1,0:T(8,128)S(1)}, u32[]{:S(2)}, u32[]{:S(2)}) collective-permute-start(f32[1,128,128]{2,1,0:T(8,128)S(1)} %get-tuple-element.132), channel_id=1, source_target_pairs={{0,103},{1,96},{2,97},{3,98},{4,99},{5,100},{6,101},{7,102},{32,71... | collective-permute-start | bytes 196616 | tf_op jit(solution)/shard_map/ppermute | solution.py:418
  446.7 7.3 %collective-permute-start.33 = (f32[1,128,128]{2,1,0:T(8,128)S(1)}, f32[1,128,128]{2,1,0:T(8,128)S(1)}, u32[]{:S(2)}, u32[]{:S(2)}) collective-permute-start(f32[1,128,128]{2,1,0:T(8,128)S(1)} %get-tuple-element.138), channel_id=1, source_target_pairs={{0,97},{1,98},{2,99},{3,100},{4,101},{5,102},{6,103},{7,96},{32,65... | collective-permute-start | bytes 196616 | tf_op jit(solution)/shard_map/ppermute | solution.py:418
  452.7 9.2 %collective-permute-start.32 = (f32[6,32,128]{2,1,0:T(8,128)S(1)}, f32[6,32,128]{2,1,0:T(8,128)S(1)}, u32[]{:S(2)}, u32[]{:S(2)}) collective-permute-start(f32[6,32,128]{2,1,0:T(8,128)S(1)} %get-tuple-element.136.refs_3_), channel_id=1, source_target_pairs={{0,16},{8,24},{16,0},{24,8},{1,17},{9,25},{17,1},{25,9},{2,18},{10... | collective-permute-start | bytes 294920 | tf_op jit(solution)/shard_map/ppermute | solution.py:17
  452.8 11.9 %collective-permute-start.31 = (f32[6,32,128]{2,1,0:T(8,128)S(1)}, f32[6,32,128]{2,1,0:T(8,128)S(1)}, u32[]{:S(2)}, u32[]{:S(2)}) collective-permute-start(f32[6,32,128]{2,1,0:T(8,128)S(1)} %get-tuple-element.136.refs_3_), channel_id=1, source_target_pairs={{0,24},{8,0},{16,8},{24,16},{1,25},{9,1},{17,9},{25,17},{2,26},{10... | collective-permute-start | bytes 294920 | tf_op jit(solution)/shard_map/ppermute | solution.py:17
  454.0 11.6 %collective-permute-start.30 = (f32[6,32,128]{2,1,0:T(8,128)S(1)}, f32[6,32,128]{2,1,0:T(8,128)S(1)}, u32[]{:S(2)}, u32[]{:S(2)}) collective-permute-start(f32[6,32,128]{2,1,0:T(8,128)S(1)} %get-tuple-element.136.refs_3_), channel_id=1, source_target_pairs={{0,8},{8,16},{16,24},{24,0},{1,9},{9,17},{17,25},{25,1},{2,10},{10... | collective-permute-start | bytes 294920 | tf_op jit(solution)/shard_map/ppermute | solution.py:17
  455.4 4.6 collective-permute-start.37
  458.3 16.1 %collective-permute-start.36 = (f32[2,16,128]{2,1,0:T(8,128)S(1)}, f32[2,16,128]{2,1,0:T(8,128)S(1)}, u32[]{:S(2)}, u32[]{:S(2)}) collective-permute-start(f32[2,16,128]{2,1,0:T(8,128)S(1)} %get-tuple-element.140.refs_2_), channel_id=1, source_target_pairs={{0,24},{8,0},{16,8},{24,16},{1,25},{9,1},{17,9},{25,17},{2,26},{10... | collective-permute-start | bytes 49160 | tf_op jit(solution)/shard_map/ppermute | solution.py:17
  460.0 14.5 %collective-permute-start.35 = (f32[2,16,128]{2,1,0:T(8,128)S(1)}, f32[2,16,128]{2,1,0:T(8,128)S(1)}, u32[]{:S(2)}, u32[]{:S(2)}) collective-permute-start(f32[2,16,128]{2,1,0:T(8,128)S(1)} %get-tuple-element.140.refs_2_), channel_id=1, source_target_pairs={{0,8},{8,16},{16,24},{24,0},{1,9},{9,17},{17,25},{25,1},{2,10},{10... | collective-permute-start | bytes 49160 | tf_op jit(solution)/shard_map/ppermute | solution.py:17
  461.9 14.0 %collective-permute-start.41 = (f32[2,16,128]{2,1,0:T(8,128)S(1)}, f32[2,16,128]{2,1,0:T(8,128)S(1)}, u32[]{:S(2)}, u32[]{:S(2)}) collective-permute-start(f32[2,16,128]{2,1,0:T(8,128)S(1)} %get-tuple-element.142.refs_2_), channel_id=1, source_target_pairs={{0,16},{8,24},{16,0},{24,8},{1,17},{9,25},{17,1},{25,9},{2,18},{10... | collective-permute-start | bytes 49160 | tf_op jit(solution)/shard_map/ppermute | solution.py:17
  464.7 11.2 %collective-permute-start.40 = (f32[2,16,128]{2,1,0:T(8,128)S(1)}, f32[2,16,128]{2,1,0:T(8,128)S(1)}, u32[]{:S(2)}, u32[]{:S(2)}) collective-permute-start(f32[2,16,128]{2,1,0:T(8,128)S(1)} %get-tuple-element.142.refs_2_), channel_id=1, source_target_pairs={{0,24},{8,0},{16,8},{24,16},{1,25},{9,1},{17,9},{25,17},{2,26},{10... | collective-permute-start | bytes 49160 | tf_op jit(solution)/shard_map/ppermute | solution.py:17
  465.7 10.3 %collective-permute-start.39 = (f32[2,16,128]{2,1,0:T(8,128)S(1)}, f32[2,16,128]{2,1,0:T(8,128)S(1)}, u32[]{:S(2)}, u32[]{:S(2)}) collective-permute-start(f32[2,16,128]{2,1,0:T(8,128)S(1)} %get-tuple-element.142.refs_2_), channel_id=1, source_target_pairs={{0,8},{8,16},{16,24},{24,0},{1,9},{9,17},{17,25},{25,1},{2,10},{10... | collective-permute-start | bytes 49160 | tf_op jit(solution)/shard_map/ppermute | solution.py:17
where the time goes:
time: 482 us; the launch traced here: 478 us
  waiting for transfers between devices  355 us (74%)
  starting transfers between devices  59.4 us (12%)
  Pallas kernels  50.3 us (10%)
  local copies, waits for them, and re-layouts  11.5 us (2%)
    ppermute x34, waiting for transfers between devices, shift(): return lax.ppermute(x, axis, [(i, (i + by) % size) for i in range(size)])  333 us
    ppermute x34, starting transfers between devices, shift(): return lax.ppermute(x, axis, [(i, (i + by) % size) for i in range(size)])  41.7 us
    pallas_call x7, Pallas kernels, grow(): pl.pallas_call(lambda *refs: grow_body(plan, last, *refs), grid=(depth //...  26.8 us
    ppermute x8, waiting for transfers between devices, relay(): return lax.ppermute(row, ('lat', 'lev'), pairs)  22.6 us
    ppermute x8, starting transfers between devices, relay(): return lax.ppermute(row, ('lat', 'lev'), pairs)  17.7 us
    unnamed x12, local copies, waits for them, and re-layouts  11.5 us
  transfers between devices with their start and end apart: 42, of which 14 were waited for; matrix products, arithmetic and copies ran while one was open for 0% of the time, Pallas kernels for 10%

commit v1 on v0

--- a/solution.py
+++ b/solution.py
@@ -9,7 +9,7 @@
 STEPS = 4
 ROWS = 8
 BAND = 4
-CUT = 16
+CUT = 24
 
 
 def shift(x, axis, by):
@@ -272,9 +272,9 @@
 def put_body(start, _, source, out, sems):
     copies = [
         pltpu.make_async_copy(
-            source.at[pl.ds(k * ROWS, ROWS)], out.at[pl.ds(start + k * ROWS, ROWS), :, 0], sems.at[k]
+            source.at[pl.ds(k * BAND, BAND)], out.at[pl.ds(start + k * BAND, BAND), :, 0], sems.at[k]
         )
-        for k in range(source.shape[0] // ROWS)
+        for k in range(source.shape[0] // BAND)
     ]
     for copy in copies:
         copy.start()
@@ -289,7 +289,7 @@
         in_specs=[pl.BlockSpec(memory_space=pltpu.HBM), pl.BlockSpec(memory_space=pltpu.VMEM)],
         out_specs=pl.BlockSpec(memory_space=pltpu.HBM),
         out_shape=jax.ShapeDtypeStruct(view.shape, view.dtype),
-        scratch_shapes=[pltpu.SemaphoreType.DMA((depth // ROWS,))],
+        scratch_shapes=[pltpu.SemaphoreType.DMA((depth // BAND,))],
         input_output_aliases={0: 0},
         compiler_params=pltpu.CompilerParams(vmem_limit_bytes=2**20),
         cost_estimate=pl.CostEstimate(flops=5_000_000, bytes_accessed=2**21, transcendentals=0),
@@ -301,12 +301,12 @@
     depth, width, _ = plane.shape
     mean, scale = scale_of(count, width, own, (s1, s2, s3), 0)
     copies = []
-    for k in range(depth // ROWS):
-        for r in range(k * ROWS, (k + 1) * ROWS):
+    for k in range(depth // BAND):
+        for r in range(k * BAND, (k + 1) * BAND):
             held[r, :, 0, :] = (plane[r] - mean[r : r + 1, :]) * scale[r : r + 1, :]
         copies.append(
             pltpu.make_async_copy(
-                held.at[pl.ds(k * ROWS, ROWS)], out.at[pl.ds(start + k * ROWS, ROWS), :, 0], sems.at[k]
+                held.at[pl.ds(k * BAND, BAND)], out.at[pl.ds(start + k * BAND, BAND), :, 0], sems.at[k]
             )
         )
         copies[-1].start()
@@ -324,7 +324,7 @@
         out_shape=jax.ShapeDtypeStruct(view.shape, view.dtype),
         scratch_shapes=[
             pltpu.VMEM((depth, width, 1, lanes), rows.dtype),
-            pltpu.SemaphoreType.DMA((depth // ROWS,)),
+            pltpu.SemaphoreType.DMA((depth // BAND,)),
         ],
         input_output_aliases={0: 0},
         compiler_params=pltpu.CompilerParams(vmem_limit_bytes=4 * 2**20),
@@ -438,7 +438,7 @@
             edge_of(lambda w, z: w.at[:, width - 1, z]),
             edge_of(lambda w, z: w.at[:, 0, z]),
         ],
-        50,
+        10,
     )
     sides = exchange(*rest)
     down = shift(send, "lev", -1)

time: 482 us -> 470 us (0.975)
    unnamed x12 -> x34, local copies, waits for them, and re-layouts: 11.5 us -> 10.1 us
  transfers between devices with their start and end apart: 42 -> 42, of which waited for: 14 -> 14; matrix products, arithmetic and copies ran while one was open for 0% -> 0% of each run, Pallas kernels for 10% -> 9%
where the time goes in v1:
time: 470 us; the launch traced here: 469 us
  waiting for transfers between devices  352 us (75%)
  starting transfers between devices  58.7 us (12%)
  Pallas kernels  46.4 us (10%)
  local copies, waits for them, and re-layouts  10.1 us (2%)
    ppermute x34, waiting for transfers between devices, shift(): return lax.ppermute(x, axis, [(i, (i + by) % size) for i in range(size)])  329 us
    ppermute x34, starting transfers between devices, shift(): return lax.ppermute(x, axis, [(i, (i + by) % size) for i in range(size)])  41.8 us
    pallas_call x7, Pallas kernels, grow(): pl.pallas_call(lambda *refs: grow_body(plan, last, *refs), grid=(depth //...  24.9 us
    ppermute x8, waiting for transfers between devices, relay(): return lax.ppermute(row, ('lat', 'lev'), pairs)  23.9 us
    ppermute x8, starting transfers between devices, relay(): return lax.ppermute(row, ('lat', 'lev'), pairs)  16.9 us
    unnamed x34, local copies, waits for them, and re-layouts  10.1 us
  transfers between devices with their start and end apart: 42, of which 14 were waited for; matrix products, arithmetic and copies ran while one was open for 0% of the time, Pallas kernels for 9%

profile of v1, /device:TPU:1, one launch (start us, length us, event | category | flops | bytes accessed | tf_op | source)
XLA Modules:
  0.0 469.0 jit_solution(13967148088232967404)
XLA Ops:
  0.7 1.7 take.3
  2.4 2.1 collective-permute-start.6
  4.6 2.3 take.2
  6.9 4.5 collective-permute-start.4
  12.4 2.3 collective-permute-start
  14.8 1.6 collective-permute-start.2
  16.4 84.1 %collective-permute-done.1.north.refs_7_.refs_16_.refs_25_ = f32[4,128,128]{2,1,0:T(8,128)S(1)} collective-permute-done((f32[4,128,128]{2,1,0:T(8,128)S(1)}, f32[4,128,128]{2,1,0:T(8,128)S(1)}, u32[]{:S(2)}, u32[]{:S(2)}) %collective-permute-start.1) | collective-permute-done | bytes 262176 | tf_op jit(solution)/shard_map/ppermute | solution.py:17
  100.5 3.8 collective-permute-start.3
  105.6 4.9 %copy-done.16 = f32[32,128,4,128]{3,2,1,0:T(4,128)S(1)} copy-done((f32[32,128,4,128]{3,2,1,0:T(4,128)S(1)}, f32[32,128,4,128]{3,2,1,0:T(4,128)}, u32[]{:S(2)}) %copy-start.16) | copy-done | bytes 8388632
  112.0 1.7 copy-done.12
  113.9 1.7 copy-done.13
  115.5 5.4 %grow.7 = (f32[32,128,128]{2,1,0:T(8,128)S(1)}, f32[32,128,128]{2,1,0:T(8,128)S(1)}, f32[32,128,128]{2,1,0:T(8,128)S(1)}, f32[3,128,128]{2,1,0:T(8,128)S(1)}, f3...) custom-call(s32[1]{0:T(128)} %bitcast.refs_1_.low.refs_0_, ...), custom_call_target="tpu_custom_call" | custom-call | flops 30000000 | bytes 12582912 | tf_op jit(solution)/shard_map/grow/pallas_call | solution.py:207
  121.3 1.7 collective-permute-start.12
  122.9 3.0 collective-permute-start.5
  126.0 2.7 collective-permute-done.5.refs_12_
  128.6 1.9 grow.8
  130.8 1.6 collective-permute-start.14
  132.5 2.7 collective-permute-start.8
  135.2 81.2 %collective-permute-done.8.south.refs_6_.refs_15_.refs_24_ = f32[4,128,128]{2,1,0:T(8,128)S(1)} collective-permute-done((f32[4,128,128]{2,1,0:T(8,128)S(1)}, f32[4,128,128]{2,1,0:T(8,128)S(1)}, u32[]{:S(2)}, u32[]{:S(2)}) %collective-permute-start.8) | collective-permute-done | bytes 262176 | tf_op jit(solution)/shard_map/ppermute | solution.py:17
  216.5 2.9 collective-permute-done.9.north.refs_7_.refs_16_.refs_25_
  219.5 1.7 collective-permute-start.13
  221.1 3.8 collective-permute-done.13.refs_29_
  225.0 1.6 copy-done.10
  226.6 4.7 grow.9
  231.7 8.6 %collective-permute-done.15.refs_11_ = f32[1,128,128]{2,1,0:T(8,128)S(1)} collective-permute-done((f32[1,128,128]{2,1,0:T(8,128)S(1)}, f32[1,128,128]{2,1,0:T(8,128)S(1)}, u32[]{:S(2)}, u32[]{:S(2)}) %collective-permute-start.15) | collective-permute-done | bytes 65568 | tf_op jit(solution)/shard_map/ppermute | solution.py:418
  240.3 1.8 grow.10
  242.5 1.6 collective-permute-start.16
  244.8 78.9 %collective-permute-done.16.south.refs_6_.refs_15_.refs_24_ = f32[4,128,128]{2,1,0:T(8,128)S(1)} collective-permute-done((f32[4,128,128]{2,1,0:T(8,128)S(1)}, f32[4,128,128]{2,1,0:T(8,128)S(1)}, u32[]{:S(2)}, u32[]{:S(2)}) %collective-permute-start.16) | collective-permute-done | bytes 262176 | tf_op jit(solution)/shard_map/ppermute | solution.py:17
  323.7 2.2 collective-permute-start.19
  326.8 5.5 %collective-permute-start.23 = (f32[1,128,128]{2,1,0:T(8,128)S(1)}, f32[1,128,128]{2,1,0:T(8,128)S(1)}, u32[]{:S(2)}, u32[]{:S(2)}) collective-permute-start(f32[1,128,128]{2,1,0:T(8,128)S(1)} %get-tuple-element.119), channel_id=1, source_target_pairs={{0,97},{1,98},{2,99},{3,100},{4,101},{5,102},{6,103},{7,96},{32,65... | collective-permute-start | bytes 196616 | tf_op jit(solution)/shard_map/ppermute | solution.py:418
  332.3 4.3 collective-permute-done.23.refs_29_
  336.6 4.8 %grow.11 = (f32[32,128,128]{2,1,0:T(8,128)S(1)}, f32[32,128,128]{2,1,0:T(8,128)S(1)}, f32[32,128,128]{2,1,0:T(8,128)S(1)}, f32[3,128,128]{2,1,0:T(8,128)S(1)}, f...) custom-call(s32[1]{0:T(128)} %bitcast.refs_1_.low.refs_0_, ...), custom_call_target="tpu_custom_call" | custom-call | flops 30000000 | bytes 12582912 | tf_op jit(solution)/shard_map/grow/pallas_call | solution.py:207
  341.8 3.0 collective-permute-start.21
  344.8 2.0 collective-permute-done.21.refs_12_
  346.8 1.9 grow.12
  348.9 1.9 collective-permute-start.34
  350.8 2.0 collective-permute-start.24
  353.0 73.5 %collective-permute-done.24.south.refs_6_.refs_15_.refs_24_.refs_5_ = f32[4,128,128]{2,1,0:T(8,128)S(1)} collective-permute-done((f32[4,128,128]{2,1,0:T(8,128)S(1)}, f32[4,128,128]{2,1,0:T(8,128)S(1)}, u32[]{:S(2)}, u32[]{:S(2)}) %collective-permute-start.24) | collective-permute-done | bytes 262176 | tf_op jit(solution)/shard_map/ppermute | solution.py:17
  426.5 5.4 %collective-permute-done.25.north.refs_7_.refs_16_.refs_25_.refs_6_ = f32[4,128,128]{2,1,0:T(8,128)S(1)} collective-permute-done((f32[4,128,128]{2,1,0:T(8,128)S(1)}, f32[4,128,128]{2,1,0:T(8,128)S(1)}, u32[]{:S(2)}, u32[]{:S(2)}) %collective-permute-start.25) | collective-permute-done | bytes 262176 | tf_op jit(solution)/shard_map/ppermute | solution.py:17
  432.7 2.8 collective-permute-start.29
  435.7 2.7 collective-permute-done.29.refs_29_
  438.4 4.5 grow.13
  442.9 2.6 collective-permute-start.31
  445.6 1.8 grow_last.2
  447.4 1.9 collective-permute-start.37
  452.5 3.7 collective-permute-start.41
  457.7 6.3 %finish.1 = (f32[32,512,128]{2,1,0:T(8,128)}, f32[32,512,128]{2,1,0:T(8,128)}) custom-call(f32[32,128,128]{2,1,0:T(8,128)S(1)} %get-tuple-element.133.refs_0_, f32[32,128,128]{2,1,0:T(8,128)S(1)} %get-tuple-element.134.refs_1_, f32[32,128,128]{2,1,0:T(8,128)S(1)} %get-tuple-element.135.refs_2_, f32[6,32,128]{2,1,0:T(8,128)S(1)} %get-tuple-element.136.refs_3_, ...), custom_call_target="tpu_custom_call" | custom-call | flops 30000000 | bytes 16777216 | tf_op jit(solution)/shard_map/finish/pallas_call | solution.py:260
  466.0 1.8 put_scaled.2.refs_0_
  (100 shorter events, 16.7 us)
Async XLA Ops:
  2.4 111.5 %collective-permute-start.6 = (f32[31,128,128]{2,1,0:T(8,128)S(1)}, f32[31,128,128]{2,1,0:T(8,128)S(1)}, u32[]{:S(2)}, u32[]{:S(2)}) collective-permute-start(f32[31,128,128]{2,1,0:T(8,128)S(1)} %bitcast.24), channel_id=1, source_target_pairs={{0,1},{1,2},{2,3},{3,4},{4,5},{5,6},{6,7},{7,0},{8,9},{9,10},{10,1... | collective-permute-start | bytes 6094856 | tf_op jit(solution)/shard_map/ppermute | solution.py:17
  4.6 100.3 %copy-start.15 = (f32[32,128,4,128]{3,2,1,0:T(4,128)S(1)}, f32[32,128,4,128]{3,2,1,0:T(4,128)}, u32[]{:S(2)}) copy-start(f32[32,128,4,128]{3,2,1,0:T(4,128)} %param.4) | copy-start | bytes 25165828
  6.9 121.7 %collective-permute-start.4 = (f32[31,128,128]{2,1,0:T(8,128)S(1)}, f32[31,128,128]{2,1,0:T(8,128)S(1)}, u32[]{:S(2)}, u32[]{:S(2)}) collective-permute-start(f32[31,128,128]{2,1,0:T(8,128)S(1)} %bitcast.25), channel_id=1, source_target_pairs={{0,7},{1,0},{2,1},{3,2},{4,3},{5,4},{6,5},{7,6},{8,15},{9,8},{10,9... | collective-permute-start | bytes 6094856 | tf_op jit(solution)/shard_map/ppermute | solution.py:17
  11.5 89.1 %collective-permute-start.1 = (f32[4,128,128]{2,1,0:T(8,128)S(1)}, f32[4,128,128]{2,1,0:T(8,128)S(1)}, u32[]{:S(2)}, u32[]{:S(2)}) collective-permute-start(f32[4,128,128]{2,1,0:T(8,128)S(1)} %bitcast.27), channel_id=1, source_target_pairs={{0,96},{32,0},{64,32},{96,64},{1,97},{33,1},{65,33},{97,65},{2,98}... | collective-permute-start | bytes 786440 | tf_op jit(solution)/shard_map/ppermute | solution.py:17
  12.4 91.9 %collective-permute-start = (f32[4,128,128]{2,1,0:T(8,128)S(1)}, f32[4,128,128]{2,1,0:T(8,128)S(1)}, u32[]{:S(2)}, u32[]{:S(2)}) collective-permute-start(f32[4,128,128]{2,1,0:T(8,128)S(1)} %bitcast.26), channel_id=1, source_target_pairs={{0,32},{32,64},{64,96},{96,0},{1,33},{33,65},{65,97},{97,1},{2,34}... | collective-permute-start | bytes 786440 | tf_op jit(solution)/shard_map/ppermute | solution.py:17
  14.8 99.0 %collective-permute-start.2 = (f32[4,32,128]{2,1,0:T(8,128)S(1)}, f32[4,32,128]{2,1,0:T(8,128)S(1)}, u32[]{:S(2)}, u32[]{:S(2)}) collective-permute-start(f32[4,32,128]{2,1,0:T(8,128)S(1)} %bitcast.29), channel_id=1, source_target_pairs={{0,8},{8,16},{16,24},{24,0},{1,9},{9,17},{17,25},{25,1},{2,10},{10... | collective-permute-start | bytes 196616 | tf_op jit(solution)/shard_map/ppermute | solution.py:17
  100.5 13.3 %collective-permute-start.3 = (f32[4,32,128]{2,1,0:T(8,128)S(1)}, f32[4,32,128]{2,1,0:T(8,128)S(1)}, u32[]{:S(2)}, u32[]{:S(2)}) collective-permute-start(f32[4,32,128]{2,1,0:T(8,128)S(1)} %bitcast.28), channel_id=1, source_target_pairs={{0,24},{8,0},{16,8},{24,16},{1,25},{9,1},{17,9},{25,17},{2,26},{10... | collective-permute-start | bytes 196616 | tf_op jit(solution)/shard_map/ppermute | solution.py:17
  104.3 9.5 %collective-permute-start.7 = (f32[1,128,128]{2,1,0:T(8,128)S(1)}, f32[1,128,128]{2,1,0:T(8,128)S(1)}, u32[]{:S(2)}, u32[]{:S(2)}) collective-permute-start(f32[1,128,128]{2,1,0:T(8,128)S(1)} %get-tuple-element.91), channel_id=1, source_target_pairs={{0,97},{1,98},{2,99},{3,100},{4,101},{5,102},{6,103},{7,96},{32,65... | collective-permute-start | bytes 196616 | tf_op jit(solution)/shard_map/ppermute | solution.py:418
  105.6 119.3 %copy-start.3 = (f32[32,128,128]{2,1,0:T(8,128)}, f32[32,128,128]{2,1,0:T(8,128)S(1)}, u32[]{:S(2)}) copy-start(f32[32,128,128]{2,1,0:T(8,128)S(1)} %get-tuple-element.74.refs_4_) | copy-start | bytes 6291460
  105.6 231.0 %copy-start.1 = (f32[32,128,128]{2,1,0:T(8,128)}, f32[32,128,128]{2,1,0:T(8,128)S(1)}, u32[]{:S(2)}) copy-start(f32[32,128,128]{2,1,0:T(8,128)S(1)} %get-tuple-element.89.refs_22_.refs_13_) | copy-start | bytes 6291460
  121.3 103.7 %collective-permute-start.12 = (f32[31,128,128]{2,1,0:T(8,128)S(1)}, f32[31,128,128]{2,1,0:T(8,128)S(1)}, u32[]{:S(2)}, u32[]{:S(2)}) collective-permute-start(f32[31,128,128]{2,1,0:T(8,128)S(1)} %shard_map.51), channel_id=1, source_target_pairs={{0,7},{1,0},{2,1},{3,2},{4,3},{5,4},{6,5},{7,6},{8,15},{9,8},{10,9... | collective-permute-start | bytes 6094856 | tf_op jit(solution)/shard_map/ppermute | solution.py:17
  122.9 5.7 %collective-permute-start.5 = (f32[1,128,128]{2,1,0:T(8,128)S(1)}, f32[1,128,128]{2,1,0:T(8,128)S(1)}, u32[]{:S(2)}, u32[]{:S(2)}) collective-permute-start(f32[1,128,128]{2,1,0:T(8,128)S(1)} %get-tuple-element.82), channel_id=1, source_target_pairs={{0,103},{1,96},{2,97},{3,98},{4,99},{5,100},{6,101},{7,102},{32,71... | collective-permute-start | bytes 196616 | tf_op jit(solution)/shard_map/ppermute | solution.py:418
  130.5 94.4 %copy-start.6 = (f32[32,128,128]{2,1,0:T(8,128)S(1)}, f32[32,128,128]{2,1,0:T(8,128)}, u32[]{:S(2)}) copy-start(f32[32,128,128]{2,1,0:T(8,128)} %copy-done.5) | copy-start | bytes 6291460
  130.5 94.4 %copy-start.8 = (f32[32,128,128]{2,1,0:T(8,128)S(1)}, f32[32,128,128]{2,1,0:T(8,128)}, u32[]{:S(2)}) copy-start(f32[32,128,128]{2,1,0:T(8,128)} %copy-done.7) | copy-start | bytes 6291460
  130.8 109.4 %collective-permute-start.14 = (f32[31,128,128]{2,1,0:T(8,128)S(1)}, f32[31,128,128]{2,1,0:T(8,128)S(1)}, u32[]{:S(2)}, u32[]{:S(2)}) collective-permute-start(f32[31,128,128]{2,1,0:T(8,128)S(1)} %shard_map.53), channel_id=1, source_target_pairs={{0,1},{1,2},{2,3},{3,4},{4,5},{5,6},{6,7},{7,0},{8,9},{9,10},{10,1... | collective-permute-start | bytes 6094856 | tf_op jit(solution)/shard_map/ppermute | solution.py:17
  132.5 83.9 %collective-permute-start.8 = (f32[4,128,128]{2,1,0:T(8,128)S(1)}, f32[4,128,128]{2,1,0:T(8,128)S(1)}, u32[]{:S(2)}, u32[]{:S(2)}) collective-permute-start(f32[4,128,128]{2,1,0:T(8,128)S(1)} %get-tuple-element.97), channel_id=1, source_target_pairs={{0,32},{32,64},{64,96},{96,0},{1,33},{33,65},{65,97},{97,1},{2,34}... | collective-permute-start | bytes 786440 | tf_op jit(solution)/shard_map/ppermute | solution.py:17
  135.2 84.3 %collective-permute-start.9 = (f32[4,128,128]{2,1,0:T(8,128)S(1)}, f32[4,128,128]{2,1,0:T(8,128)S(1)}, u32[]{:S(2)}, u32[]{:S(2)}) collective-permute-start(f32[4,128,128]{2,1,0:T(8,128)S(1)} %get-tuple-element.98), channel_id=1, source_target_pairs={{0,96},{32,0},{64,32},{96,64},{1,97},{33,1},{65,33},{97,65},{2,98}... | collective-permute-start | bytes 786440 | tf_op jit(solution)/shard_map/ppermute | solution.py:17
  135.2 85.9 %collective-permute-start.10 = (f32[4,32,128]{2,1,0:T(8,128)S(1)}, f32[4,32,128]{2,1,0:T(8,128)S(1)}, u32[]{:S(2)}, u32[]{:S(2)}) collective-permute-start(f32[4,32,128]{2,1,0:T(8,128)S(1)} %get-tuple-element.99), channel_id=1, source_target_pairs={{0,8},{8,16},{16,24},{24,0},{1,9},{9,17},{17,25},{25,1},{2,10},{10... | collective-permute-start | bytes 196616 | tf_op jit(solution)/shard_map/ppermute | solution.py:17
  216.4 4.7 %collective-permute-start.11 = (f32[4,32,128]{2,1,0:T(8,128)S(1)}, f32[4,32,128]{2,1,0:T(8,128)S(1)}, u32[]{:S(2)}, u32[]{:S(2)}) collective-permute-start(f32[4,32,128]{2,1,0:T(8,128)S(1)} %get-tuple-element.100), channel_id=1, source_target_pairs={{0,24},{8,0},{16,8},{24,16},{1,25},{9,1},{17,9},{25,17},{2,26},{10... | collective-permute-start | bytes 196616 | tf_op jit(solution)/shard_map/ppermute | solution.py:17
  219.5 5.5 %collective-permute-start.13 = (f32[1,128,128]{2,1,0:T(8,128)S(1)}, f32[1,128,128]{2,1,0:T(8,128)S(1)}, u32[]{:S(2)}, u32[]{:S(2)}) collective-permute-start(f32[1,128,128]{2,1,0:T(8,128)S(1)} %get-tuple-element.104), channel_id=1, source_target_pairs={{0,103},{1,96},{2,97},{3,98},{4,99},{5,100},{6,101},{7,102},{32,71... | collective-permute-start | bytes 196616 | tf_op jit(solution)/shard_map/ppermute | solution.py:418
  231.5 105.1 %collective-permute-start.22 = (f32[31,128,128]{2,1,0:T(8,128)S(1)}, f32[31,128,128]{2,1,0:T(8,128)S(1)}, u32[]{:S(2)}, u32[]{:S(2)}) collective-permute-start(f32[31,128,128]{2,1,0:T(8,128)S(1)} %shard_map.56), channel_id=1, source_target_pairs={{0,1},{1,2},{2,3},{3,4},{4,5},{5,6},{6,7},{7,0},{8,9},{9,10},{10,1... | collective-permute-start | bytes 6094856 | tf_op jit(solution)/shard_map/ppermute | solution.py:17
  231.6 8.7 %collective-permute-start.15 = (f32[1,128,128]{2,1,0:T(8,128)S(1)}, f32[1,128,128]{2,1,0:T(8,128)S(1)}, u32[]{:S(2)}, u32[]{:S(2)}) collective-permute-start(f32[1,128,128]{2,1,0:T(8,128)S(1)} %get-tuple-element.106), channel_id=1, source_target_pairs={{0,97},{1,98},{2,99},{3,100},{4,101},{5,102},{6,103},{7,96},{32,65... | collective-permute-start | bytes 196616 | tf_op jit(solution)/shard_map/ppermute | solution.py:418
  242.4 104.4 %collective-permute-start.20 = (f32[31,128,128]{2,1,0:T(8,128)S(1)}, f32[31,128,128]{2,1,0:T(8,128)S(1)}, u32[]{:S(2)}, u32[]{:S(2)}) collective-permute-start(f32[31,128,128]{2,1,0:T(8,128)S(1)} %shard_map.54), channel_id=1, source_target_pairs={{0,7},{1,0},{2,1},{3,2},{4,3},{5,4},{6,5},{7,6},{8,15},{9,8},{10,9... | collective-permute-start | bytes 6094856 | tf_op jit(solution)/shard_map/ppermute | solution.py:17
  242.5 81.2 %collective-permute-start.16 = (f32[4,128,128]{2,1,0:T(8,128)S(1)}, f32[4,128,128]{2,1,0:T(8,128)S(1)}, u32[]{:S(2)}, u32[]{:S(2)}) collective-permute-start(f32[4,128,128]{2,1,0:T(8,128)S(1)} %get-tuple-element.111), channel_id=1, source_target_pairs={{0,32},{32,64},{64,96},{96,0},{1,33},{33,65},{65,97},{97,1},{2,34}... | collective-permute-start | bytes 786440 | tf_op jit(solution)/shard_map/ppermute | solution.py:17
  244.1 82.7 %collective-permute-start.17 = (f32[4,128,128]{2,1,0:T(8,128)S(1)}, f32[4,128,128]{2,1,0:T(8,128)S(1)}, u32[]{:S(2)}, u32[]{:S(2)}) collective-permute-start(f32[4,128,128]{2,1,0:T(8,128)S(1)} %get-tuple-element.112), channel_id=1, source_target_pairs={{0,96},{32,0},{64,32},{96,64},{1,97},{33,1},{65,33},{97,65},{2,98}... | collective-permute-start | bytes 786440 | tf_op jit(solution)/shard_map/ppermute | solution.py:17
  244.1 88.2 %collective-permute-start.18 = (f32[4,32,128]{2,1,0:T(8,128)S(1)}, f32[4,32,128]{2,1,0:T(8,128)S(1)}, u32[]{:S(2)}, u32[]{:S(2)}) collective-permute-start(f32[4,32,128]{2,1,0:T(8,128)S(1)} %get-tuple-element.113), channel_id=1, source_target_pairs={{0,8},{8,16},{16,24},{24,0},{1,9},{9,17},{17,25},{25,1},{2,10},{10... | collective-permute-start | bytes 196616 | tf_op jit(solution)/shard_map/ppermute | solution.py:17
  323.7 8.6 %collective-permute-start.19 = (f32[4,32,128]{2,1,0:T(8,128)S(1)}, f32[4,32,128]{2,1,0:T(8,128)S(1)}, u32[]{:S(2)}, u32[]{:S(2)}) collective-permute-start(f32[4,32,128]{2,1,0:T(8,128)S(1)} %get-tuple-element.114), channel_id=1, source_target_pairs={{0,24},{8,0},{16,8},{24,16},{1,25},{9,1},{17,9},{25,17},{2,26},{10... | collective-permute-start | bytes 196616 | tf_op jit(solution)/shard_map/ppermute | solution.py:17
  326.8 9.8 %collective-permute-start.23 = (f32[1,128,128]{2,1,0:T(8,128)S(1)}, f32[1,128,128]{2,1,0:T(8,128)S(1)}, u32[]{:S(2)}, u32[]{:S(2)}) collective-permute-start(f32[1,128,128]{2,1,0:T(8,128)S(1)} %get-tuple-element.119), channel_id=1, source_target_pairs={{0,97},{1,98},{2,99},{3,100},{4,101},{5,102},{6,103},{7,96},{32,65... | collective-permute-start | bytes 196616 | tf_op jit(solution)/shard_map/ppermute | solution.py:418
  341.7 96.7 %collective-permute-start.28 = (f32[31,128,128]{2,1,0:T(8,128)S(1)}, f32[31,128,128]{2,1,0:T(8,128)S(1)}, u32[]{:S(2)}, u32[]{:S(2)}) collective-permute-start(f32[31,128,128]{2,1,0:T(8,128)S(1)} %shard_map.57), channel_id=1, source_target_pairs={{0,7},{1,0},{2,1},{3,2},{4,3},{5,4},{6,5},{7,6},{8,15},{9,8},{10,9... | collective-permute-start | bytes 6094856 | tf_op jit(solution)/shard_map/ppermute | solution.py:17
  341.8 5.0 %collective-permute-start.21 = (f32[1,128,128]{2,1,0:T(8,128)S(1)}, f32[1,128,128]{2,1,0:T(8,128)S(1)}, u32[]{:S(2)}, u32[]{:S(2)}) collective-permute-start(f32[1,128,128]{2,1,0:T(8,128)S(1)} %get-tuple-element.117), channel_id=1, source_target_pairs={{0,103},{1,96},{2,97},{3,98},{4,99},{5,100},{6,101},{7,102},{32,71... | collective-permute-start | bytes 196616 | tf_op jit(solution)/shard_map/ppermute | solution.py:418
  348.9 89.4 %copy-start.2 = (f32[32,128,128]{2,1,0:T(8,128)S(1)}, f32[32,128,128]{2,1,0:T(8,128)}, u32[]{:S(2)}) copy-start(f32[32,128,128]{2,1,0:T(8,128)} %copy-done.1) | copy-start | bytes 6291460
  348.9 96.6 %collective-permute-start.34 = (f32[24,128,128]{2,1,0:T(8,128)S(1)}, f32[24,128,128]{2,1,0:T(8,128)S(1)}, u32[]{:S(2)}, u32[]{:S(2)}) collective-permute-start(f32[24,128,128]{2,1,0:T(8,128)S(1)} %shard_map.59), channel_id=1, source_target_pairs={{0,1},{1,2},{2,3},{3,4},{4,5},{5,6},{6,7},{7,0},{8,9},{9,10},{10,1... | collective-permute-start | bytes 4718600 | tf_op jit(solution)/shard_map/ppermute | solution.py:17
  350.8 75.7 %collective-permute-start.24 = (f32[4,128,128]{2,1,0:T(8,128)S(1)}, f32[4,128,128]{2,1,0:T(8,128)S(1)}, u32[]{:S(2)}, u32[]{:S(2)}) collective-permute-start(f32[4,128,128]{2,1,0:T(8,128)S(1)} %get-tuple-element.125), channel_id=1, source_target_pairs={{0,32},{32,64},{64,96},{96,0},{1,33},{33,65},{65,97},{97,1},{2,34}... | collective-permute-start | bytes 786440 | tf_op jit(solution)/shard_map/ppermute | solution.py:17
  352.9 79.1 %collective-permute-start.25 = (f32[4,128,128]{2,1,0:T(8,128)S(1)}, f32[4,128,128]{2,1,0:T(8,128)S(1)}, u32[]{:S(2)}, u32[]{:S(2)}) collective-permute-start(f32[4,128,128]{2,1,0:T(8,128)S(1)} %get-tuple-element.126), channel_id=1, source_target_pairs={{0,96},{32,0},{64,32},{96,64},{1,97},{33,1},{65,33},{97,65},{2,98}... | collective-permute-start | bytes 786440 | tf_op jit(solution)/shard_map/ppermute | solution.py:17
  352.9 96.3 %collective-permute-start.38 = (f32[7,128,128]{2,1,0:T(8,128)S(1)}, f32[7,128,128]{2,1,0:T(8,128)S(1)}, u32[]{:S(2)}, u32[]{:S(2)}) collective-permute-start(f32[7,128,128]{2,1,0:T(8,128)S(1)} %shard_map.60), channel_id=1, source_target_pairs={{0,1},{1,2},{2,3},{3,4},{4,5},{5,6},{6,7},{7,0},{8,9},{9,10},{10,1... | collective-permute-start | bytes 1376264 | tf_op jit(solution)/shard_map/ppermute | solution.py:17
  426.5 6.2 %collective-permute-start.26 = (f32[4,32,128]{2,1,0:T(8,128)S(1)}, f32[4,32,128]{2,1,0:T(8,128)S(1)}, u32[]{:S(2)}, u32[]{:S(2)}) collective-permute-start(f32[4,32,128]{2,1,0:T(8,128)S(1)} %get-tuple-element.127), channel_id=1, source_target_pairs={{0,8},{8,16},{16,24},{24,0},{1,9},{9,17},{17,25},{25,1},{2,10},{10... | collective-permute-start | bytes 196616 | tf_op jit(solution)/shard_map/ppermute | solution.py:17
  431.9 3.6 collective-permute-start.27
  432.7 5.7 %collective-permute-start.29 = (f32[1,128,128]{2,1,0:T(8,128)S(1)}, f32[1,128,128]{2,1,0:T(8,128)S(1)}, u32[]{:S(2)}, u32[]{:S(2)}) collective-permute-start(f32[1,128,128]{2,1,0:T(8,128)S(1)} %get-tuple-element.132), channel_id=1, source_target_pairs={{0,103},{1,96},{2,97},{3,98},{4,99},{5,100},{6,101},{7,102},{32,71... | collective-permute-start | bytes 196616 | tf_op jit(solution)/shard_map/ppermute | solution.py:418
  435.5 10.1 %collective-permute-start.33 = (f32[1,128,128]{2,1,0:T(8,128)S(1)}, f32[1,128,128]{2,1,0:T(8,128)S(1)}, u32[]{:S(2)}, u32[]{:S(2)}) collective-permute-start(f32[1,128,128]{2,1,0:T(8,128)S(1)} %get-tuple-element.138), channel_id=1, source_target_pairs={{0,97},{1,98},{2,99},{3,100},{4,101},{5,102},{6,103},{7,96},{32,65... | collective-permute-start | bytes 196616 | tf_op jit(solution)/shard_map/ppermute | solution.py:418
  442.9 9.6 %collective-permute-start.32 = (f32[6,32,128]{2,1,0:T(8,128)S(1)}, f32[6,32,128]{2,1,0:T(8,128)S(1)}, u32[]{:S(2)}, u32[]{:S(2)}) collective-permute-start(f32[6,32,128]{2,1,0:T(8,128)S(1)} %get-tuple-element.136.refs_3_), channel_id=1, source_target_pairs={{0,16},{8,24},{16,0},{24,8},{1,17},{9,25},{17,1},{25,9},{2,18},{10... | collective-permute-start | bytes 294920 | tf_op jit(solution)/shard_map/ppermute | solution.py:17
  442.9 13.3 %collective-permute-start.31 = (f32[6,32,128]{2,1,0:T(8,128)S(1)}, f32[6,32,128]{2,1,0:T(8,128)S(1)}, u32[]{:S(2)}, u32[]{:S(2)}) collective-permute-start(f32[6,32,128]{2,1,0:T(8,128)S(1)} %get-tuple-element.136.refs_3_), channel_id=1, source_target_pairs={{0,24},{8,0},{16,8},{24,16},{1,25},{9,1},{17,9},{25,17},{2,26},{10... | collective-permute-start | bytes 294920 | tf_op jit(solution)/shard_map/ppermute | solution.py:17
  445.6 10.6 %collective-permute-start.30 = (f32[6,32,128]{2,1,0:T(8,128)S(1)}, f32[6,32,128]{2,1,0:T(8,128)S(1)}, u32[]{:S(2)}, u32[]{:S(2)}) collective-permute-start(f32[6,32,128]{2,1,0:T(8,128)S(1)} %get-tuple-element.136.refs_3_), channel_id=1, source_target_pairs={{0,8},{8,16},{16,24},{24,0},{1,9},{9,17},{17,25},{25,1},{2,10},{10... | collective-permute-start | bytes 294920 | tf_op jit(solution)/shard_map/ppermute | solution.py:17
  447.4 4.4 collective-permute-start.37
  449.2 16.7 %collective-permute-start.36 = (f32[2,24,128]{2,1,0:T(8,128)S(1)}, f32[2,24,128]{2,1,0:T(8,128)S(1)}, u32[]{:S(2)}, u32[]{:S(2)}) collective-permute-start(f32[2,24,128]{2,1,0:T(8,128)S(1)} %get-tuple-element.140.refs_2_), channel_id=1, source_target_pairs={{0,24},{8,0},{16,8},{24,16},{1,25},{9,1},{17,9},{25,17},{2,26},{10... | collective-permute-start | bytes 73736 | tf_op jit(solution)/shard_map/ppermute | solution.py:17
  451.7 14.3 %collective-permute-start.35 = (f32[2,24,128]{2,1,0:T(8,128)S(1)}, f32[2,24,128]{2,1,0:T(8,128)S(1)}, u32[]{:S(2)}, u32[]{:S(2)}) collective-permute-start(f32[2,24,128]{2,1,0:T(8,128)S(1)} %get-tuple-element.140.refs_2_), channel_id=1, source_target_pairs={{0,8},{8,16},{16,24},{24,0},{1,9},{9,17},{17,25},{25,1},{2,10},{10... | collective-permute-start | bytes 73736 | tf_op jit(solution)/shard_map/ppermute | solution.py:17
  452.5 15.3 %collective-permute-start.41 = (f32[2,8,128]{2,1,0:T(8,128)S(1)}, f32[2,8,128]{2,1,0:T(8,128)S(1)}, u32[]{:S(2)}, u32[]{:S(2)}) collective-permute-start(f32[2,8,128]{2,1,0:T(8,128)S(1)} %get-tuple-element.142.refs_2_), channel_id=1, source_target_pairs={{0,16},{8,24},{16,0},{24,8},{1,17},{9,25},{17,1},{25,9},{2,18},{10... | collective-permute-start | bytes 24584 | tf_op jit(solution)/shard_map/ppermute | solution.py:17
  456.2 11.6 %collective-permute-start.40 = (f32[2,8,128]{2,1,0:T(8,128)S(1)}, f32[2,8,128]{2,1,0:T(8,128)S(1)}, u32[]{:S(2)}, u32[]{:S(2)}) collective-permute-start(f32[2,8,128]{2,1,0:T(8,128)S(1)} %get-tuple-element.142.refs_2_), channel_id=1, source_target_pairs={{0,24},{8,0},{16,8},{24,16},{1,25},{9,1},{17,9},{25,17},{2,26},{10... | collective-permute-start | bytes 24584 | tf_op jit(solution)/shard_map/ppermute | solution.py:17
  456.2 11.6 %collective-permute-start.39 = (f32[2,8,128]{2,1,0:T(8,128)S(1)}, f32[2,8,128]{2,1,0:T(8,128)S(1)}, u32[]{:S(2)}, u32[]{:S(2)}) collective-permute-start(f32[2,8,128]{2,1,0:T(8,128)S(1)} %get-tuple-element.142.refs_2_), channel_id=1, source_target_pairs={{0,8},{8,16},{16,24},{24,0},{1,9},{9,17},{17,25},{25,1},{2,10},{10... | collective-permute-start | bytes 24584 | tf_op jit(solution)/shard_map/ppermute | solution.py:17
  (11 other events, 59.7 us)
